TPU v7x, 32 devices: a whole 2x2x4 slice. The times are simulated.
32 devices in a mesh: rows: 8 (over y, x, core), cols: 4 (over z).
Axes of the slice: x: 2, y: 2, z: 4, core: 2. Of those that a mesh axis runs over, the one named last changes fastest.
Arguments:
- density: bfloat16 [640, 640], P('rows', 'cols'), as said below
- occupancy: int32 [5, 5], replicated, may hold values from 0 to 1, as said below
- square_filter: int32 [5, 5], replicated, may hold values 0 or 1
- cube_filter: int32 [5, 5], replicated, may hold values 0 or 1
Outputs:
- purified: float32 [640, 640], P('rows', 'cols')
Inputs may be any that keep to these rules, and one draw needn't show every extreme that they name: density is symmetric. occupancy is symmetric and every diagonal tile is stored.
All inputs are finite; a program needn't handle non-finite values.
Results may differ from a plain program's by a relative error of at most 0.0095.
Values may be sent and summed in bfloat16 or wider, within the bound.
No kernel may reach another device: no remote copies, remote signals or barrier semaphores. Data moves between devices by JAX's collectives and lax.ppermute only.
A program may use at most 64 MiB of HBM per device.

v0:
```python
import jax
import jax.numpy as jnp
from jax import lax
from jax.sharding import PartitionSpec as P

TILE = 128


def expand(table, row_start, row_count, col_start, col_count):
    count = table.shape[0]
    tile_ids = jnp.arange(count, dtype=jnp.int32)
    row_tiles = (jnp.arange(row_count, dtype=jnp.int32) + row_start) // TILE
    col_tiles = (jnp.arange(col_count, dtype=jnp.int32) + col_start) // TILE
    row_pick = (row_tiles[:, None] == tile_ids[None, :]).astype(jnp.float32)
    col_pick = (tile_ids[:, None] == col_tiles[None, :]).astype(jnp.float32)
    left = jnp.dot(row_pick, table.astype(jnp.float32), precision=lax.Precision.HIGHEST)
    return jnp.dot(left, col_pick, precision=lax.Precision.HIGHEST)


def over_panel(step, init, occupied):
    return step(init, lax.all_gather(occupied, "rows", axis=0, tiled=True), jnp.int32(0))


def on_device(density, occupancy, square_filter, cube_filter):
    row_count, col_count = density.shape
    row_start = lax.axis_index("rows") * row_count
    col_start = lax.axis_index("cols") * col_count
    stored_mask = expand(occupancy, row_start, row_count, col_start, col_count)
    square_mask = expand(square_filter, row_start, row_count, col_start, col_count)
    cube_mask = expand(cube_filter, row_start, row_count, col_start, col_count)
    occupied = jnp.where(stored_mask > 0.5, density, jnp.zeros_like(density))
    empty = jnp.zeros((row_count, col_count), jnp.float32)
    panel = lax.all_gather(occupied, "cols", axis=1, tiled=True)

    def add_square(total, piece, start):
        return jnp.dot(panel, piece, preferred_element_type=jnp.float32)

    square_total = over_panel(add_square, empty, occupied)
    square = jnp.where(square_mask > 0.5, square_total, 0.0).astype(jnp.bfloat16)
    square_rows = lax.all_gather(square, "cols", axis=1, tiled=True)

    def add_cube(total, piece, start):
        return jnp.dot(square_rows, piece, preferred_element_type=jnp.float32)

    cube_total = over_panel(add_cube, empty, occupied)
    cube = jnp.where(cube_mask > 0.5, cube_total, 0.0)
    return 3.0 * square.astype(jnp.float32) - 2.0 * cube


def solution(mesh):
    placed = (P("rows", "cols"), P(), P(), P())
    return jax.shard_map(
        on_device, mesh=mesh, in_specs=placed, out_specs=P("rows", "cols"), check_vma=False
    )
```

profile of v0, /device:TPU:0, one launch (start us, length us, event | category | flops | bytes accessed | tf_op | source)
XLA Modules:
  0.0 42.6 jit_solution(16775872245500241807)
XLA Ops:
  0.0 0.0 copy-start
  0.0 0.9 %fusion.5 = f32[80,5]{1,0:T(8,128)S(1)} fusion(s32[80]{0:T(128)S(1)} %and_select_fusion.1, s32[5,5]{1,0:T(8,128)} %param.5), kind=kOutput, calls=%fused_computation.11 | convolution fusion | flops 24425 | bytes 2020 | tf_op jit(solution)/shard_map/dot_general | solution.py:16
  0.9 0.0 copy-done
  0.9 0.2 fusion.3
  1.1 0.0 copy-start.1
  1.1 0.1 copy.5
  1.2 0.6 %copy-done.1 = s32[5,5]{1,0:T(8,128)S(1)} copy-done((s32[5,5]{1,0:T(8,128)S(1)}, s32[5,5]{1,0:T(8,128)}, u32[]{:S(2)}) %copy-start.1) | copy-done | bytes 124
  1.8 0.2 fusion.6
  2.0 0.0 copy-start.2
  2.0 0.2 convolution_compare_fusion.2
  2.2 0.5 %copy-done.2 = s32[5,5]{1,0:T(8,128)S(1)} copy-done((s32[5,5]{1,0:T(8,128)S(1)}, s32[5,5]{1,0:T(8,128)}, u32[]{:S(2)}) %copy-start.2) | copy-done | bytes 124
  2.7 0.2 fusion.4
  2.9 0.2 convolution_compare_fusion
  3.1 15.2 %all_gather.10 = bf16[80,640]{0,1:T(8,128)(2,1)S(1)} all-gather(bf16[80,160]{0,1:T(8,128)(2,1)S(1)} %copy.5), channel_id=1, replica_groups=mesh['rows'=8,'cols'=4] {'cols'}, dimensions={1}, use_global_device_ids=true | all-gather | bytes 128000 | tf_op jit(solution)/shard_map/all_gather | solution.py:33
  18.3 9.4 %all_gather.11 = bf16[640,160]{1,0:T(8,128)(2,1)S(1)} all-gather(bf16[80,160]{1,0:T(8,128)(2,1)S(1)} %fusion.3), channel_id=1, replica_groups=mesh['rows'=8,'cols'=4] {'rows'}, dimensions={0}, use_global_device_ids=true | all-gather | bytes 230400 | tf_op jit(solution)/shard_map/all_gather | solution.py:21
  27.7 0.2 fusion.2
  27.9 0.1 copy.6
  28.0 13.7 %all_gather.12 = bf16[80,640]{0,1:T(8,128)(2,1)S(1)} all-gather(bf16[80,160]{0,1:T(8,128)(2,1)S(1)} %copy.6), channel_id=1, replica_groups=mesh['rows'=8,'cols'=4] {'cols'}, dimensions={1}, use_global_device_ids=true | all-gather | bytes 128000 | tf_op jit(solution)/shard_map/all_gather | solution.py:40
  41.7 0.9 %fusion.1 = f32[80,160]{1,0:T(8,128)} fusion(pred[80,160]{1,0:T(8,128)(4,1)S(1)} %convolution_compare_fusion, bf16[80,640]{0,1:T(8,128)(2,1)S(1)} %all_gather.12, bf16[640,160]{1,0:T(8,128)(2,1)S(1)} %all_gather.11, bf16[80,160]{1,0:T(8,128)(2,1)S(1)} %fusion.2), kind=kOutput, calls=%fused_computation.3 | convolution fusion | flops 16448000 | bytes 396800 | tf_op jit(solution)/shard_map/dot_general | solution.py:43
  (2 shorter events, 0.0 us)
Async XLA Ops:
  0.0 0.9 %copy-start = (bf16[80,160]{1,0:T(8,128)(2,1)S(1)}, bf16[80,160]{1,0:T(8,128)(2,1)}, u32[]{:S(2)}) copy-start(bf16[80,160]{1,0:T(8,128)(2,1)} %param.4) | copy-start | bytes 76804
  1.1 0.7 %copy-start.1 = (s32[5,5]{1,0:T(8,128)S(1)}, s32[5,5]{1,0:T(8,128)}, u32[]{:S(2)}) copy-start(s32[5,5]{1,0:T(8,128)} %param.6) | copy-start | bytes 304
  2.0 0.7 %copy-start.2 = (s32[5,5]{1,0:T(8,128)S(1)}, s32[5,5]{1,0:T(8,128)}, u32[]{:S(2)}) copy-start(s32[5,5]{1,0:T(8,128)} %param.7) | copy-start | bytes 304
where the time goes:
time: 42.9 us; the launch traced here: 42.6 us
  blocking collectives  38.3 us (89%)
  matrix products  2.92 us (7%)
  local copies, waits for them, and re-layouts  1.3 us (3%)
    all_gather x1, blocking collectives, on_device(): panel = lax.all_gather(occupied, 'cols', axis=1, tiled=True)  15.2 us
    all_gather x1, blocking collectives, on_device(): square_rows = lax.all_gather(square, 'cols', axis=1, tiled=True)  13.7 us
    all_gather x1, blocking collectives, over_panel(): lax.all_gather(occupied, 'rows', axis=0, tiled=True)  9.43 us
    dot_general x3, matrix products, expand(): jnp.dot(row_pick, table.astype(jnp.float32), precision=lax.Precision.HIGH...  1.33 us
    unnamed x6, local copies, waits for them, and re-layouts  1.08 us
    dot_general x1, matrix products, add_cube(): return jnp.dot(square_rows, piece, preferred_element_type=jnp.float32)  0.86 us

commit v1 on v0

--- a/solution.py
+++ b/solution.py
@@ -30,7 +30,12 @@
     cube_mask = expand(cube_filter, row_start, row_count, col_start, col_count)
     occupied = jnp.where(stored_mask > 0.5, density, jnp.zeros_like(density))
     empty = jnp.zeros((row_count, col_count), jnp.float32)
-    panel = lax.all_gather(occupied, "cols", axis=1, tiled=True)
+    ring = [occupied]
+    for hop in range(3):
+        ring.append(lax.ppermute(ring[-1], "cols", [(dev, (dev + 1) % 4) for dev in range(4)]))
+    panel = jnp.roll(
+        jnp.concatenate(ring[::-1], axis=1), (lax.axis_index("cols") + 1) * ring[0].shape[1], axis=1
+    )
 
     def add_square(total, piece, start):
         return jnp.dot(panel, piece, preferred_element_type=jnp.float32)

time: 42.9 us -> 39 us (0.909)
  blocking collectives: 38.3 us -> 23.4 us
  waiting for transfers between devices: 0 us -> 8.49 us
  starting transfers between devices: 0 us -> 3.11 us
  local copies, waits for them, and re-layouts: 1.3 us -> 0.79 us
    all_gather x1 -> x0, blocking collectives: 15.2 us -> none  [on_device(): panel = lax.all_gather(occupied, 'cols', axis=1, tiled=True)]
    ppermute x0 -> x3, waiting for transfers between devices: none -> 8.49 us  [on_device(): lax.ppermute(ring[-1], 'cols', [(dev, (dev + 1) % 4) for dev in range(4)])]
    ppermute x0 -> x3, starting transfers between devices: none -> 3.11 us  [on_device(): lax.ppermute(ring[-1], 'cols', [(dev, (dev + 1) % 4) for dev in range(4)])]
    unnamed x6, local copies, waits for them, and re-layouts: 1.08 us -> 0.52 us
  transfers between devices with their start and end apart: 0 -> 3, of which waited for: 0 -> 2; matrix products, arithmetic and copies ran while one was open for 0% -> 2% of each run, Pallas kernels for 0% -> 0%
where the time goes in v1:
time: 39 us; the launch traced here: 38.8 us
  blocking collectives  23.4 us (60%)
  waiting for transfers between devices  8.49 us (22%)
  starting transfers between devices  3.11 us (8%)
  matrix products  2.93 us (8%)
  local copies, waits for them, and re-layouts  0.79 us (2%)
    all_gather x1, blocking collectives, on_device(): square_rows = lax.all_gather(square, 'cols', axis=1, tiled=True)  13.7 us
    all_gather x1, blocking collectives, over_panel(): lax.all_gather(occupied, 'rows', axis=0, tiled=True)  9.65 us
    ppermute x3, waiting for transfers between devices, on_device(): lax.ppermute(ring[-1], 'cols', [(dev, (dev + 1) % 4) for dev in range(4)])  8.49 us
    ppermute x3, starting transfers between devices, on_device(): lax.ppermute(ring[-1], 'cols', [(dev, (dev + 1) % 4) for dev in range(4)])  3.11 us
    dot_general x3, matrix products, expand(): jnp.dot(row_pick, table.astype(jnp.float32), precision=lax.Precision.HIGH...  1.33 us
    dot_general x1, matrix products, add_cube(): return jnp.dot(square_rows, piece, preferred_element_type=jnp.float32)  0.86 us
  transfers between devices with their start and end apart: 3, of which 2 were waited for; matrix products, arithmetic and copies ran while one was open for 2% of the time, Pallas kernels for 0%

profile of v1, /device:TPU:0, one launch (start us, length us, event | category | flops | bytes accessed | tf_op | source)
XLA Modules:
  0.0 38.8 jit_solution(16996158427087671239)
XLA Ops:
  0.0 0.0 copy-start
  0.0 0.9 %fusion.6 = f32[80,5]{1,0:T(8,128)S(1)} fusion(s32[80]{0:T(128)S(1)} %and_select_fusion.1, s32[5,5]{1,0:T(8,128)} %param.5), kind=kOutput, calls=%fused_computation.12 | convolution fusion | flops 24425 | bytes 2020 | tf_op jit(solution)/shard_map/dot_general | solution.py:16
  0.9 0.0 copy-done
  0.9 0.0 copy-start.1
  1.0 0.2 fusion.3
  1.1 3.1 %collective-permute-start = (bf16[80,160]{1,0:T(8,128)(2,1)S(1)}, bf16[80,160]{1,0:T(8,128)(2,1)S(1)}, u32[]{:S(2)}, u32[]{:S(2)}) collective-permute-start(bf16[80,160]{1,0:T(8,128)(2,1)S(1)} %fusion.3), channel_id=1, source_target_pairs={{0,1},{1,2},{2,3},{3,0},{4,5},{5,6},{6,7},{7,4},{8,9},{9,10},{10,1... | collective-permute-start | bytes 76808 | tf_op jit(solution)/shard_map/ppermute | solution.py:35
  4.2 0.0 copy-done.1
  4.2 0.2 fusion.7
  4.5 0.0 copy-start.2
  4.5 0.2 convolution_compare_fusion.2
  4.6 0.5 %copy-done.2 = s32[5,5]{1,0:T(8,128)S(1)} copy-done((s32[5,5]{1,0:T(8,128)S(1)}, s32[5,5]{1,0:T(8,128)}, u32[]{:S(2)}) %copy-start.2) | copy-done | bytes 124
  5.1 0.2 fusion.5
  5.4 2.9 %collective-permute-done = bf16[80,160]{1,0:T(8,128)(2,1)S(1)} collective-permute-done((bf16[80,160]{1,0:T(8,128)(2,1)S(1)}, bf16[80,160]{1,0:T(8,128)(2,1)S(1)}, u32[]{:S(2)}, u32[]{:S(2)}) %collective-permute-start) | collective-permute-done | bytes 25632 | tf_op jit(solution)/shard_map/ppermute | solution.py:35
  8.2 0.0 collective-permute-start.1
  8.2 0.2 convolution_compare_fusion
  8.4 5.6 %collective-permute-done.1 = bf16[80,160]{1,0:T(8,128)(2,1)S(1)} collective-permute-done((bf16[80,160]{1,0:T(8,128)(2,1)S(1)}, bf16[80,160]{1,0:T(8,128)(2,1)S(1)}, u32[]{:S(2)}, u32[]{:S(2)}) %collective-permute-start.1) | collective-permute-done | bytes 25632 | tf_op jit(solution)/shard_map/ppermute | solution.py:35
  14.0 0.0 collective-permute-start.2
  14.0 9.6 %all_gather.7 = bf16[640,160]{1,0:T(8,128)(2,1)S(1)} all-gather(bf16[80,160]{1,0:T(8,128)(2,1)S(1)} %fusion.3), channel_id=1, replica_groups=mesh['rows'=8,'cols'=4] {'rows'}, dimensions={0}, use_global_device_ids=true | all-gather | bytes 230400 | tf_op jit(solution)/shard_map/all_gather | solution.py:21
  23.7 0.0 collective-permute-done.2
  23.7 0.2 concatenate.6
  23.9 0.2 fusion.2
  24.1 0.1 copy.5
  24.2 13.7 %all_gather.8 = bf16[80,640]{0,1:T(8,128)(2,1)S(1)} all-gather(bf16[80,160]{0,1:T(8,128)(2,1)S(1)} %copy.5), channel_id=1, replica_groups=mesh['rows'=8,'cols'=4] {'cols'}, dimensions={1}, use_global_device_ids=true | all-gather | bytes 128000 | tf_op jit(solution)/shard_map/all_gather | solution.py:45
  37.9 0.9 %fusion.1 = f32[80,160]{1,0:T(8,128)} fusion(pred[80,160]{1,0:T(8,128)(4,1)S(1)} %convolution_compare_fusion, bf16[80,640]{0,1:T(8,128)(2,1)S(1)} %all_gather.8, bf16[640,160]{1,0:T(8,128)(2,1)S(1)} %all_gather.7, bf16[80,160]{1,0:T(8,128)(2,1)S(1)} %fusion.2), kind=kOutput, calls=%fused_computation.3 | convolution fusion | flops 16448000 | bytes 396800 | tf_op jit(solution)/shard_map/dot_general | solution.py:48
  (2 shorter events, 0.0 us)
Async XLA Ops:
  0.0 0.9 %copy-start = (bf16[80,160]{1,0:T(8,128)(2,1)S(1)}, bf16[80,160]{1,0:T(8,128)(2,1)}, u32[]{:S(2)}) copy-start(bf16[80,160]{1,0:T(8,128)(2,1)} %param.4) | copy-start | bytes 76804
  0.9 3.3 %copy-start.1 = (s32[5,5]{1,0:T(8,128)S(1)}, s32[5,5]{1,0:T(8,128)}, u32[]{:S(2)}) copy-start(s32[5,5]{1,0:T(8,128)} %param.6) | copy-start | bytes 304
  1.1 7.1 %collective-permute-start = (bf16[80,160]{1,0:T(8,128)(2,1)S(1)}, bf16[80,160]{1,0:T(8,128)(2,1)S(1)}, u32[]{:S(2)}, u32[]{:S(2)}) collective-permute-start(bf16[80,160]{1,0:T(8,128)(2,1)S(1)} %fusion.3), channel_id=1, source_target_pairs={{0,1},{1,2},{2,3},{3,0},{4,5},{5,6},{6,7},{7,4},{8,9},{9,10},{10,1... | collective-permute-start | bytes 76808 | tf_op jit(solution)/shard_map/ppermute | solution.py:35
  4.5 0.7 %copy-start.2 = (s32[5,5]{1,0:T(8,128)S(1)}, s32[5,5]{1,0:T(8,128)}, u32[]{:S(2)}) copy-start(s32[5,5]{1,0:T(8,128)} %param.7) | copy-start | bytes 304
  8.2 5.8 %collective-permute-start.1 = (bf16[80,160]{1,0:T(8,128)(2,1)S(1)}, bf16[80,160]{1,0:T(8,128)(2,1)S(1)}, u32[]{:S(2)}, u32[]{:S(2)}) collective-permute-start(bf16[80,160]{1,0:T(8,128)(2,1)S(1)} %collective-permute-done), channel_id=1, source_target_pairs={{0,1},{1,2},{2,3},{3,0},{4,5},{5,6},{6,7},{7,4},{8,9},{9,10},{10,1... | collective-permute-start | bytes 76808 | tf_op jit(solution)/shard_map/ppermute | solution.py:35
  14.0 9.7 %collective-permute-start.2 = (bf16[80,160]{1,0:T(8,128)(2,1)S(1)}, bf16[80,160]{1,0:T(8,128)(2,1)S(1)}, u32[]{:S(2)}, u32[]{:S(2)}) collective-permute-start(bf16[80,160]{1,0:T(8,128)(2,1)S(1)} %collective-permute-done.1), channel_id=1, source_target_pairs={{0,1},{1,2},{2,3},{3,0},{4,5},{5,6},{6,7},{7,4},{8,9},{9,10},{10,1... | collective-permute-start | bytes 76808 | tf_op jit(solution)/shard_map/ppermute | solution.py:35
